TPU v7x, 32 devices: a whole 2x2x4 slice. The times are simulated.
32 devices in a mesh: groups: 2 (over y), seq: 4 (over z), tensor: 2 (over x), cfg: 2 (over core).
Axes of the slice: x: 2, y: 2, z: 4, core: 2. Of those that a mesh axis runs over, the one named last changes fastest.
Arguments:
- latent: bfloat16 [2048, 3072], P(('groups', 'seq')), parts along dimension 0, may hold values from -6 to 6
- positions: int32 [3, 2048], P(None, ('groups', 'seq')), parts along dimension 1, may hold values from 0 to 79, as said below
- text_kv: bfloat16 [2, 2, 128, 3072], P('cfg', None, ('groups', 'seq'), 'tensor'), parts along dimension 2, may hold values from -6 to 6
- text_len: int32 [4], P(('groups', 'cfg')), parts along dimension 0, may hold values from 1 to 64
- modulation: float32 [3, 4, 3072], P(None, 'groups'), parts along dimension 1, may hold values from -3 to 3
- w_qkv: bfloat16 [3, 3072, 3072], P(None, 'cfg', 'tensor'), may hold values from -0.109375 to 0.109375
- norm_gains: float32 [2, 128], replicated, may hold values from 0.5 to 2.5
- w_out: bfloat16 [3072, 3072], P('tensor', 'cfg'), may hold values from -0.109375 to 0.109375
- guidance: float32 [2], P('groups'), parts along dimension 0, may hold values from 3 to 8
Outputs:
- guided: bfloat16 [2048, 3072], P(('groups', 'seq', 'tensor'), 'cfg'), parts along dimension 0
There are 2 independent parts, one for each index of `groups`. A program takes and returns all parts, laid end to end along the dimension named above; an argument that names none is the same for every part. Nothing has to cross between parts.
Inputs may be any that keep to these rules, and one draw needn't show every extreme that they name: `positions`: frame indices are below 33, height indices below 45, width indices below 80. `text_len`: text rows at or beyond the count are ignored.
All inputs are finite; a program needn't handle non-finite values.
Results may differ from a plain program's by a relative error of at most 0.018.
Values may be sent and summed in bfloat16 or wider, within the bound.
A program may use at most 128 MiB of HBM per device.

v0:
```python
import jax
import jax.numpy as jnp
from jax import lax
from jax.sharding import PartitionSpec as P

HEAD_DIM = 128


def swapped(value, axis, apart):
    mask = 2**apart
    pairs = [(source, source ^ mask) for source in range(lax.axis_size(axis))]
    return lax.ppermute(value, axis, pairs)


def head_norm(heads_in, gain):
    return (
        heads_in * lax.rsqrt(jnp.mean(heads_in * heads_in, axis=-1, keepdims=True) + 1e-06) * gain
    )


def rotary(heads_in, positions):
    head_size = heads_in.shape[-1]
    blocks = (head_size // 8, 7 * head_size // 16, 7 * head_size // 16)
    pieces = []
    offset = 0
    for axis_id in range(3):
        width = blocks[axis_id]
        half = width // 2
        freq = 256.0 ** (-jnp.arange(half, dtype=jnp.float32) / half)
        angle = positions[axis_id].astype(jnp.float32)[:, None] * freq[None, :]
        cosine = jnp.cos(angle)[:, None, :]
        sine = jnp.sin(angle)[:, None, :]
        first = heads_in[..., offset : offset + half]
        second = heads_in[..., offset + half : offset + width]
        pieces.append(first * cosine - second * sine)
        pieces.append(second * cosine + first * sine)
        offset = offset + width
    return jnp.concatenate(pieces, axis=-1)


def local(latent, positions, text_kv, text_len, modulation, w_qkv, norm_gains, w_out, guidance):
    rows_here = latent.shape[0]
    width_dev = w_qkv.shape[2]
    heads_dev = width_dev // HEAD_DIM
    text_dev = text_kv.shape[2]
    branch = lax.axis_index("cfg")
    xfloat = latent.astype(jnp.float32)
    center = xfloat - jnp.mean(xfloat, axis=-1, keepdims=True)
    normed = center * lax.rsqrt(jnp.mean(center * center, axis=-1, keepdims=True) + 1e-06)
    both_mod = (
        normed[None] * (1.0 + modulation[1][:, None, :]) + modulation[0][:, None, :]
    ).astype(jnp.bfloat16)
    rows_w = w_qkv.shape[1]
    columns = lax.dynamic_slice_in_dim(both_mod, branch * rows_w, rows_w, 2)
    terms = jnp.einsum("btd,jde->bjte", columns, w_qkv, preferred_element_type=jnp.float32)
    projected = lax.psum_scatter(
        terms.astype(jnp.bfloat16), "cfg", scatter_dimension=0, tiled=True
    ).astype(jnp.float32)[0]
    queries = rotary(
        head_norm(projected[0].reshape(rows_here, heads_dev, HEAD_DIM), norm_gains[0]), positions
    ).astype(jnp.bfloat16)
    keys = rotary(
        head_norm(projected[1].reshape(rows_here, heads_dev, HEAD_DIM), norm_gains[1]), positions
    ).astype(jnp.bfloat16)
    keys = keys.reshape(rows_here, width_dev)
    value_rows = projected[2].astype(jnp.bfloat16)
    text_raw = text_kv[0, 0].astype(jnp.float32).reshape(text_dev, heads_dev, HEAD_DIM)
    text_keys = head_norm(text_raw, norm_gains[1]).astype(jnp.bfloat16).reshape(text_dev, width_dev)
    text_values = text_kv[0, 1]
    length = text_len[0]
    scale = HEAD_DIM ** (-0.5)

    def attend(carry, key_rows, val_rows, valid):
        running_sum, accum = carry
        count = key_rows.shape[0]
        key_heads = key_rows.reshape(count, heads_dev, HEAD_DIM)
        val_heads = val_rows.reshape(count, heads_dev, HEAD_DIM)
        scores = (
            jnp.einsum("thd,nhd->htn", queries, key_heads, preferred_element_type=jnp.float32)
            * scale
        )
        expo = jnp.where(valid[None, None, :], jnp.exp(scores), 0.0)
        new_sum = running_sum + jnp.sum(expo, axis=-1)
        new_acc = accum + jnp.einsum(
            "htn,nhd->htd", expo.astype(jnp.bfloat16), val_heads, preferred_element_type=jnp.float32
        )
        return (new_sum, new_acc)

    start_state = (
        jnp.zeros((heads_dev, rows_here), jnp.float32),
        jnp.zeros((heads_dev, rows_here, HEAD_DIM), jnp.float32),
    )
    carry = start_state
    image_keys = lax.all_gather(keys, "seq", axis=0, tiled=True)
    image_values = lax.all_gather(value_rows, "seq", axis=0, tiled=True)
    prompt_keys = lax.all_gather(text_keys, "seq", axis=0, tiled=True)
    prompt_values = lax.all_gather(text_values, "seq", axis=0, tiled=True)
    carry = attend(carry, image_keys, image_values, jnp.ones((image_keys.shape[0],), bool))
    text_index = jnp.arange(prompt_keys.shape[0], dtype=jnp.int32)
    state = attend(carry, prompt_keys, prompt_values, text_index < length)
    final_sum, final_acc = state
    attended = (
        (final_acc / final_sum[..., None])
        .transpose(1, 0, 2)
        .reshape(rows_here, width_dev)
        .astype(jnp.bfloat16)
    )
    strength = guidance[0]
    half_cols = w_out.shape[1]
    full_out = lax.all_gather(w_out, "cfg", axis=1, tiled=True)
    summed = lax.psum_scatter(
        jnp.dot(attended, full_out, preferred_element_type=jnp.float32).astype(jnp.bfloat16),
        "tensor",
        scatter_dimension=0,
        tiled=True,
    ).astype(jnp.float32)
    gate = lax.dynamic_index_in_dim(modulation[2], branch, 0, keepdims=False)
    mine = (gate * summed).astype(jnp.bfloat16)
    own_half = lax.dynamic_slice_in_dim(mine, branch * half_cols, half_cols, 1)
    send_half = lax.dynamic_slice_in_dim(mine, (1 - branch) * half_cols, half_cols, 1)
    other = swapped(send_half, "cfg", 0)
    cond_rows = jnp.where(branch == 0, own_half, other).astype(jnp.float32)
    uncond_rows = jnp.where(branch == 0, other, own_half).astype(jnp.float32)
    guided = (uncond_rows + strength * (cond_rows - uncond_rows)).astype(jnp.bfloat16)
    return guided


def solution(mesh):
    placed = (
        P(("groups", "seq"), None),
        P(None, ("groups", "seq")),
        P("cfg", None, ("groups", "seq"), "tensor"),
        P(("groups", "cfg")),
        P(None, "groups", None),
        P(None, "cfg", "tensor"),
        P(),
        P("tensor", "cfg"),
        P("groups"),
    )
    return jax.shard_map(
        local,
        mesh=mesh,
        in_specs=placed,
        out_specs=P(("groups", "seq", "tensor"), "cfg"),
        check_vma=False,
    )
```

profile of v0, /device:TPU:0, one launch (start us, length us, event | category | flops | bytes accessed | tf_op | source)
XLA Modules:
  0.0 247.0 jit_solution(18201941797049536414)
XLA Ops:
  6.5 1.5 fusion.31
  8.1 1.7 convert_reduce_fusion
  9.8 0.6 fusion.11
  10.3 2.3 fusion.9
  12.6 1.5 constant_dynamic-slice_fusion.1
  14.1 14.2 %convert_bitcast_fusion = bf16[2,3,256,1536]{3,2,1,0:T(8,128)(2,1)} fusion(bf16[3,1536,1536]{2,1,0:T(8,128)(2,1)} %param.14, f32[2,1536]{1,0:T(2,128)S(1)} %get-tuple-element.46, f32[2,1536]{1,0:T(2,128)S(1)} %get-tuple-element.45, f32[256,1536]{1,0:T(8,128)S(1)} %constant_dynamic-slice_fusion.1), kind=kOutput, calls=%fused_computation.7 | convolution fusion | flops 7252475904 | bytes 20471808 | tf_op jit(solution)/shard_map/btd,jde->bjte/dot_general | solution.py:55
  28.3 0.0 reduce-scatter.3.cloned.1.call-update
  28.3 0.0 copy-start.11
  28.3 0.0 copy-start.12
  28.3 0.0 all-gather.10.cloned.1.call-start
  28.4 15.3 %reduce-scatter.3.cloned.1.call-done = bf16[1,3,256,1536]{3,2,1,0:T(8,128)(2,1)} async-done(((bf16[2,3,256,1536]{3,2,1,0:T(8,128)(2,1)}), bf16[1,3,256,1536]{3,2,1,0:T(8,128)(2,1)}) %reduce-scatter.3.cloned.1.call-update) | async-done | bytes 2359312 | tf_op jit(solution)/shard_map/reduce_scatter | solution.py:56
  43.7 2.3 slice.122
  46.0 0.0 all-gather.10.cloned.1.call-update
  46.0 0.0 all-gather.6.cloned.1.call-start
  46.1 0.1 multiply_cosine_fusion.2
  46.2 0.8 copy.24
  47.0 0.8 copy.25
  47.8 1.5 multiply_cosine_fusion
  49.4 2.0 fusion.30
  51.4 1.9 copy.22
  53.3 1.6 copy.23
  54.9 2.0 copy.26
  56.9 1.6 copy.27
  58.5 0.1 multiply_reduce_fusion.1
  58.7 0.1 multiply_reduce_fusion
  58.8 1.1 copy-done.2
  60.0 0.5 multiply_multiply_fusion.1
  60.4 0.9 copy-done.3
  61.4 0.5 multiply_multiply_fusion
  61.8 0.4 copy-done.5
  62.3 3.3 %add_convert_fusion.1 = (bf16[256,12,28]{2,0,1:T(8,128)(2,1)}, bf16[256,12,28]{2,0,1:T(8,128)(2,1)}, bf16[256,12,28]{2,0,1:T(8,128)(2,1)}, bf16[256,12,28]{2,0,1:T(8,128)(2,1)}) fusion(f32[256,12,128]{2,0,1:T(8,128)S(1)} %multiply_multiply_fusion, f32[256,28]{1,0:T(8,128)S(1)} %get-tuple-element.32, f32[256,28]{1,0:T(8,128)S(1)} %get-tuple-element.31, ...), kind=kLoop, calls=%fused_computation.22 | loop fusion | flops 1376256 | bytes 2179072 | tf_op jit(solution)/shard_map/convert.7
  65.6 2.3 add_convert_fusion.3
  67.9 5.8 %concatenate.9 = bf16[256,12,128]{2,0,1:T(8,128)(2,1)} concatenate(bf16[256,12,8]{2,0,1:T(8,128)(2,1)} %get-tuple-element.12, bf16[256,12,8]{2,0,1:T(8,128)(2,1)} %get-tuple-element.11, bf16[256,12,28]{2,0,1:T(8,128)(2,1)} %get-tuple-element.19, bf16[256,12,28]{2,0,1:T(8,128)(2,1)} %get-tuple-element.20, bf16[256,12,28]{2,0,1:T(8,128)(2,1)} %get-tuple-element.8, ...), dimensions={2} | concatenate | bytes 1572864 | tf_op jit(solution)/shard_map/concatenate | solution.py:38
  73.7 2.3 copy.28
  76.0 0.0 all-gather.6.cloned.1.call-update
  76.0 0.0 all-gather.8.cloned.1.call-start
  76.1 0.5 all-gather.8.cloned.1.call-update
  76.6 0.0 reduce-scatter.5.cloned.1.call-start
  76.7 1.4 slice.107
  78.1 1.4 convert_multiply_fusion
  79.5 1.6 mul.442
  81.8 17.6 %all-gather.1 = bf16[1,1,64,1536]{3,2,1,0:T(8,128)(2,1)} all-gather(bf16[1,1,16,1536]{3,2,1,0:T(8,128)(2,1)} %slice.107), channel_id=3, replica_groups=mesh['groups'=2,'seq'=4,'tensor'=2,'cfg'=2] {'seq'}, dimensions={2}, use_global_device_ids=true | all-gather | bytes 245760 | tf_op jit(solution)/shard_map/all_gather | solution.py:97
  99.4 1.8 reshape.268
  101.2 1.0 reduce_sum.67
  102.2 0.1 mul.443
  102.3 0.8 fusion.28
  103.1 15.8 %all_gather.17 = bf16[64,1536]{1,0:T(8,128)(2,1)} all-gather(bf16[16,1536]{1,0:T(8,128)(2,1)S(1)} %fusion.28), channel_id=1, replica_groups=mesh['groups'=2,'seq'=4,'tensor'=2,'cfg'=2] {'seq'}, dimensions={0}, use_global_device_ids=true | all-gather | bytes 245760 | tf_op jit(solution)/shard_map/all_gather | solution.py:96
  118.9 4.2 %add_convert_fusion.4 = (bf16[256,12,28]{2,0,1:T(8,128)(2,1)}, bf16[256,12,28]{2,0,1:T(8,128)(2,1)}, bf16[256,12,28]{2,0,1:T(8,128)(2,1)}, bf16[256,12,28]{2,0,1:T(8,128)(2,1)}) fusion(f32[256,12,128]{2,0,1:T(8,128)S(1)} %multiply_multiply_fusion.1, f32[256,28]{1,0:T(8,128)S(1)} %get-tuple-element.32, f32[256,28]{1,0:T(8,128)S(1)} %get-tuple-element.31, ...), kind=kLoop, calls=%fused_computation.30 | loop fusion | flops 1376256 | bytes 2179072 | tf_op jit(solution)/shard_map/convert.13
  123.2 4.6 %concatenate.8 = bf16[256,12,128]{2,0,1:T(8,128)(2,1)S(1)} concatenate(bf16[256,12,8]{2,0,1:T(8,128)(2,1)S(1)} %get-tuple-element.23, bf16[256,12,8]{2,0,1:T(8,128)(2,1)S(1)} %get-tuple-element.24, bf16[256,12,28]{2,0,1:T(8,128)(2,1)} %get-tuple-element.21, bf16[256,12,28]{2,0,1:T(8,128)(2,1)} %get-tuple-element.22, bf16[256,12,28]{2,0,1:T(8,128)(2,1)} %get-tuple-element.14, ...), dimensions={2} | concatenate | bytes 1572864 | tf_op jit(solution)/shard_map/concatenate | solution.py:38
  127.8 1.2 fusion.32
  129.0 4.7 %copy.30 = bf16[1,1,1024,1536]{2,3,1,0:T(8,128)(2,1)} copy(bf16[1,1,1024,1536]{3,2,1,0:T(8,128)(2,1)} %all-gather.10.cloned.1.call-done) | data formatting | bytes 6291456 | tf_op jit(solution)/shard_map/all_gather | solution.py:95
  133.7 46.5 %all-gather.6.cloned.1.call-done = bf16[1024,1536]{0,1:T(8,128)(2,1)} async-done(((bf16[256,1536]{0,1:T(8,128)(2,1)}), bf16[1024,1536]{0,1:T(8,128)(2,1)}) %all-gather.6.cloned.1.call-update) | async-done | bytes 3145744 | tf_op jit(solution)/shard_map/all_gather | solution.py:94
  180.2 4.1 %fusion.2 = (f32[12,256]{1,0:T(8,128)S(1)}, f32[12,256,1024]{2,1,0:T(8,128)S(1)}) fusion(bf16[256,12,128]{2,0,1:T(8,128)(2,1)} %copy-done.4, bf16[1024,12,128]{0,2,1:T(8,128)(2,1)} %bitcast.78), kind=kOutput, calls=%fused_computation.3 | convolution fusion | flops 811594752 | bytes 16527360 | tf_op jit(solution)/shard_map/thd,nhd->htn/dot_general | solution.py:79
  184.4 5.6 %fusion.4 = f32[12,256,128]{1,2,0:T(8,128)} fusion(bf16[1024,12,128]{0,2,1:T(8,128)(2,1)} %bitcast.77, f32[12,256,1024]{2,1,0:T(8,128)S(1)} %get-tuple-element.42), kind=kOutput, calls=%fused_computation.5 | convolution fusion | flops 811597824 | bytes 17301504 | tf_op jit(solution)/shard_map/htn,nhd->htd/dot_general | solution.py:84
  190.0 2.4 fusion.17
  192.4 9.1 %all-gather.8.cloned.1.call-done = bf16[1536,3072]{1,0:T(8,128)(2,1)} async-done(((bf16[1536,1536]{1,0:T(8,128)(2,1)}), bf16[1536,3072]{1,0:T(8,128)(2,1)}) %all-gather.8.cloned.1.call-update) | async-done | bytes 9437200 | tf_op jit(solution)/shard_map/all_gather | solution.py:110
  201.5 7.4 %convolution_convert_fusion = bf16[256,3072]{1,0:T(8,128)(2,1)} fusion(bf16[256,1536]{0,1:T(8,128)(2,1)S(1)} %bitcast.80, bf16[1536,3072]{1,0:T(8,128)(2,1)} %all-gather.8.cloned.1.call-done), kind=kOutput, calls=%fused_computation.10 | convolution fusion | flops 2416705536 | bytes 11796480 | tf_op jit(solution)/shard_map/dot_general | solution.py:112
  208.9 0.0 reduce-scatter.5.cloned.1.call-update
  208.9 0.7 copy-done.10
  209.7 26.7 %reduce-scatter.5.cloned.1.call-done = bf16[128,3072]{1,0:T(8,128)(2,1)} async-done(((bf16[256,3072]{1,0:T(8,128)(2,1)}), bf16[128,3072]{1,0:T(8,128)(2,1)}) %reduce-scatter.5.cloned.1.call-update) | async-done | bytes 786448 | tf_op jit(solution)/shard_map/reduce_scatter | solution.py:111
  236.4 1.3 multiply_convert_fusion
  237.7 0.1 collective-permute-start
  238.5 1.1 collective-permute-done
  239.5 0.9 fusion.21
  (37 shorter events, 0.2 us)
Async XLA Ops:
  6.5 3.2 %copy-start = (bf16[256,3072]{1,0:T(8,128)(2,1)S(1)}, bf16[256,3072]{1,0:T(8,128)(2,1)}, u32[]{:S(2)}) copy-start(bf16[256,3072]{1,0:T(8,128)(2,1)} %param.9) | copy-start | bytes 4718596
  6.5 37.2 %reduce-scatter.3.cloned.1.call-start = ((), (), s32[]{:S(2)}) async-start(), calls=%async_computation.2 | async-start | bytes 7077888 | tf_op jit(solution)/shard_map/reduce_scatter | solution.py:56
  28.3 17.8 %copy-start.11 = (s32[3,256]{1,0:T(4,128)S(1)}, s32[3,256]{1,0:T(4,128)}, u32[]{:S(2)}) copy-start(s32[3,256]{1,0:T(4,128)} %param.10) | copy-start | bytes 9220
  28.3 19.5 %copy-start.12 = (f32[2,128]{1,0:T(2,128)S(1)}, f32[2,128]{1,0:T(2,128)}, u32[]{:S(2)}) copy-start(f32[2,128]{1,0:T(2,128)} %param.15) | copy-start | bytes 3076
  28.3 100.7 %all-gather.10.cloned.1.call-start = ((), (), s32[]{:S(2)}) async-start(), calls=%async_computation.6 | async-start | bytes 3932160 | tf_op jit(solution)/shard_map/all_gather | solution.py:95
  43.7 5.7 %copy-start.1 = (bf16[1,3,256,1536]{3,2,1,0:T(8,128)(2,1)S(1)}, bf16[1,3,256,1536]{3,2,1,0:T(8,128)(2,1)}, u32[]{:S(2)}) copy-start(bf16[1,3,256,1536]{3,2,1,0:T(8,128)(2,1)} %reduce-scatter.3.cloned.1.call-done) | copy-start | bytes 7077892
  46.0 134.2 %all-gather.6.cloned.1.call-start = ((), (), s32[]{:S(2)}) async-start(), calls=%async_computation.3 | async-start | bytes 3932160 | tf_op jit(solution)/shard_map/all_gather | solution.py:94
  58.5 1.4 copy-start.2
  60.0 1.4 copy-start.3
  61.4 0.9 copy-start.5
  62.3 3.3 %copy-start.6 = (f32[256,8]{1,0:T(8,128)S(1)}, f32[256,8]{1,0:T(8,128)}, u32[]{:S(2)}) copy-start(f32[256,8]{1,0:T(8,128)} %copy.24) | copy-start | bytes 24580
  62.3 3.3 %copy-start.7 = (f32[256,8]{1,0:T(8,128)S(1)}, f32[256,8]{1,0:T(8,128)}, u32[]{:S(2)}) copy-start(f32[256,8]{1,0:T(8,128)} %copy.25) | copy-start | bytes 24580
  76.0 125.4 %all-gather.8.cloned.1.call-start = ((), (), s32[]{:S(2)}) async-start(), calls=%async_computation.4 | async-start | bytes 14155776 | tf_op jit(solution)/shard_map/all_gather | solution.py:110
  76.6 159.8 %reduce-scatter.5.cloned.1.call-start = ((), (), s32[]{:S(2)}) async-start(), calls=%async_computation.5 | async-start | bytes 2359296 | tf_op jit(solution)/shard_map/reduce_scatter | solution.py:111
  123.2 4.6 %copy-start.9 = (bf16[64,1536]{1,0:T(8,128)(2,1)S(1)}, bf16[64,1536]{1,0:T(8,128)(2,1)}, u32[]{:S(2)}) copy-start(bf16[64,1536]{1,0:T(8,128)(2,1)} %all_gather.17) | copy-start | bytes 589828
  127.8 5.9 %copy-start.4 = (bf16[256,12,128]{2,0,1:T(8,128)(2,1)}, bf16[256,12,128]{2,0,1:T(8,128)(2,1)S(1)}, u32[]{:S(2)}) copy-start(bf16[256,12,128]{2,0,1:T(8,128)(2,1)S(1)} %concatenate.8) | copy-start | bytes 2359300
  184.4 5.6 %copy-start.8 = (bf16[64,12,128]{2,1,0:T(8,128)(2,1)S(1)}, bf16[64,12,128]{2,1,0:T(8,128)(2,1)}, u32[]{:S(2)}) copy-start(bf16[64,12,128]{2,1,0:T(8,128)(2,1)} %reshape.268) | copy-start | bytes 589828
  208.9 0.7 copy-start.10
  237.7 1.8 collective-permute-start
Sparse Core Ops, SparseCore 0:
  28.4 15.2 reduce-scatter.2
  46.1 70.3 all-gather.9
  118.1 62.0 all-gather.5
  181.6 19.7 all-gather.7
  209.0 27.3 reduce-scatter.4
where the time goes:
time: 248 us; the launch traced here: 247 us
  waiting for transfers between devices  99.3 us (40%)
  local copies, waits for them, and re-layouts  40.1 us (16%)
  matrix products  34.9 us (14%)
  blocking collectives  33.4 us (13%)
  other arithmetic  24.3 us (10%)
  between operations  14.7 us (6%)
    all_gather x1, waiting for transfers between devices, local(): image_keys = lax.all_gather(keys, 'seq', axis=0, tiled=True)  46.5 us
    reduce_scatter x1, waiting for transfers between devices, local(): lax.psum_scatter(jnp.dot(attended, full_out, preferred_element_type=jnp.f...  26.7 us
    all_gather x1, blocking collectives, local(): prompt_values = lax.all_gather(text_values, 'seq', axis=0, tiled=True)  17.6 us
    all_gather x1, blocking collectives, local(): prompt_keys = lax.all_gather(text_keys, 'seq', axis=0, tiled=True)  15.8 us
    reduce_scatter x1, waiting for transfers between devices, local(): lax.psum_scatter(terms.astype(jnp.bfloat16), 'cfg', scatter_dimension=0,...  15.3 us
    dot_general x1, matrix products, local(): jnp.einsum('btd,jde->bjte', columns, w_qkv, preferred_element_type=jnp.fl...  14.2 us
    concatenate x3, local copies, waits for them, and re-layouts, rotary(): return jnp.concatenate(pieces, axis=-1)  12.8 us
    another operation x3, other arithmetic  9.86 us
  transfers between devices with their start and end apart: 6, of which 5 were waited for; matrix products, arithmetic and copies ran while one was open for 25% of the time, Pallas kernels for 0%

commit v1 on v0

--- a/solution.py
+++ b/solution.py
@@ -91,8 +91,11 @@
         jnp.zeros((heads_dev, rows_here, HEAD_DIM), jnp.float32),
     )
     carry = start_state
-    image_keys = lax.all_gather(keys, "seq", axis=0, tiled=True)
-    image_values = lax.all_gather(value_rows, "seq", axis=0, tiled=True)
+    image_keys, image_values = jnp.split(
+        lax.all_gather(jnp.concatenate([keys, value_rows], axis=1), "seq", axis=0, tiled=True),
+        [keys.shape[1]],
+        axis=1,
+    )
     prompt_keys = lax.all_gather(text_keys, "seq", axis=0, tiled=True)
     prompt_values = lax.all_gather(text_values, "seq", axis=0, tiled=True)
     carry = attend(carry, image_keys, image_values, jnp.ones((image_keys.shape[0],), bool))

time: 248 us -> 259 us (1.044)
  waiting for transfers between devices: 99.3 us -> 109 us
  blocking collectives: 33.4 us -> 36 us
    all_gather x2 -> x1, waiting for transfers between devices: 46.5 us -> 71.4 us  [local(): lax.all_gather(jnp.concatenate([keys, value_rows], axis=1), 'seq', axis=0...]
    split x0 -> x3, local copies, waits for them, and re-layouts: none -> 12.8 us  [local(): jnp.split(lax.all_gather(jnp.concatenate([keys, value_rows], axis=1), 'se...]
    all_gather x1, waiting for transfers between devices: 9.06 us -> 0.02 us  [local(): full_out = lax.all_gather(w_out, 'cfg', axis=1, tiled=True)]
    all_gather x1, blocking collectives: 15.8 us -> 21 us  [local(): prompt_keys = lax.all_gather(text_keys, 'seq', axis=0, tiled=True)]
    all_gather x1 -> x0, local copies, waits for them, and re-layouts: 4.69 us -> none  [local(): image_values = lax.all_gather(value_rows, 'seq', axis=0, tiled=True)]
    reduce_scatter x1, waiting for transfers between devices: 15.3 us -> 11 us  [local(): lax.psum_scatter(terms.astype(jnp.bfloat16), 'cfg', scatter_dimension=0,...]
    all_gather x1, blocking collectives: 17.6 us -> 15 us  [local(): prompt_values = lax.all_gather(text_values, 'seq', axis=0, tiled=True)]
  transfers between devices with their start and end apart: 6 -> 5, of which waited for: 5 -> 4; matrix products, arithmetic and copies ran while one was open for 25% -> 15% of each run, Pallas kernels for 0% -> 0%
where the time goes in v1:
time: 259 us; the launch traced here: 258 us
  waiting for transfers between devices  109 us (42%)
  local copies, waits for them, and re-layouts  41 us (16%)
  blocking collectives  36 us (14%)
  matrix products  34.3 us (13%)
  other arithmetic  22.6 us (9%)
  between operations  14.8 us (6%)
    all_gather x1, waiting for transfers between devices, local(): lax.all_gather(jnp.concatenate([keys, value_rows], axis=1), 'seq', axis=0...  71.4 us
    reduce_scatter x1, waiting for transfers between devices, local(): lax.psum_scatter(jnp.dot(attended, full_out, preferred_element_type=jnp.f...  25 us
    all_gather x1, blocking collectives, local(): prompt_keys = lax.all_gather(text_keys, 'seq', axis=0, tiled=True)  21 us
    all_gather x1, blocking collectives, local(): prompt_values = lax.all_gather(text_values, 'seq', axis=0, tiled=True)  15 us
    dot_general x1, matrix products, local(): jnp.einsum('btd,jde->bjte', columns, w_qkv, preferred_element_type=jnp.fl...  14.1 us
    split x3, local copies, waits for them, and re-layouts, local(): jnp.split(lax.all_gather(jnp.concatenate([keys, value_rows], axis=1), 'se...  12.8 us
    concatenate x3, local copies, waits for them, and re-layouts, rotary(): return jnp.concatenate(pieces, axis=-1)  11.4 us
    reduce_scatter x1, waiting for transfers between devices, local(): lax.psum_scatter(terms.astype(jnp.bfloat16), 'cfg', scatter_dimension=0,...  11 us
  transfers between devices with their start and end apart: 5, of which 4 were waited for; matrix products, arithmetic and copies ran while one was open for 15% of the time, Pallas kernels for 0%

profile of v1, /device:TPU:0, one launch (start us, length us, event | category | flops | bytes accessed | tf_op | source)
XLA Modules:
  0.0 258.1 jit_solution(16085171058808939353)
XLA Ops:
  6.5 1.5 fusion.32
  8.0 1.7 convert_reduce_fusion
  9.8 0.6 fusion.11
  10.3 2.3 fusion.9
  12.6 1.5 constant_dynamic-slice_fusion.1
  14.1 14.1 %convert_bitcast_fusion = bf16[2,3,256,1536]{3,2,1,0:T(8,128)(2,1)} fusion(bf16[3,1536,1536]{2,1,0:T(8,128)(2,1)} %param.14, f32[2,1536]{1,0:T(2,128)S(1)} %get-tuple-element.48, f32[2,1536]{1,0:T(2,128)S(1)} %get-tuple-element.47, f32[256,1536]{1,0:T(8,128)S(1)} %constant_dynamic-slice_fusion.1), kind=kOutput, calls=%fused_computation.7 | convolution fusion | flops 7252475904 | bytes 20471808 | tf_op jit(solution)/shard_map/btd,jde->bjte/dot_general | solution.py:55
  28.3 0.0 reduce-scatter.3.cloned.1.call-update
  28.3 0.0 all-gather.4.cloned.1.call-start
  28.4 0.6 copy-done.13
  29.0 0.1 multiply_cosine_fusion.2
  29.1 0.8 copy.29
  29.9 0.8 copy.28
  30.7 0.6 slice_bitcast_fusion.3
  31.3 1.5 multiply_cosine_fusion
  32.8 11.0 %reduce-scatter.3.cloned.1.call-done = bf16[1,3,256,1536]{3,2,1,0:T(8,128)(2,1)} async-done(((bf16[2,3,256,1536]{3,2,1,0:T(8,128)(2,1)}), bf16[1,3,256,1536]{3,2,1,0:T(8,128)(2,1)}) %reduce-scatter.3.cloned.1.call-update) | async-done | bytes 2359312 | tf_op jit(solution)/shard_map/reduce_scatter | solution.py:56
  43.7 2.9 %fusion.31 = (f32[1,1,256,1536]{3,2,1,0:T(8,128)S(1)}, f32[1,1,256,1536]{3,2,1,0:T(8,128)}) fusion(bf16[1,3,256,1536]{3,2,1,0:T(8,128)(2,1)} %reduce-scatter.3.cloned.1.call-done), kind=kLoop, calls=%fused_computation.86 | loop fusion | bytes 6291456 | tf_op jit(solution)/shard_map/slice | solution.py:60
  46.7 0.5 copy.26
  47.2 0.5 copy.27
  47.6 0.1 multiply_reduce_fusion.1
  47.8 1.9 copy.30
  49.7 1.6 copy.31
  51.3 0.1 multiply_reduce_fusion
  51.5 0.5 copy-done.14
  51.9 0.5 multiply_multiply_fusion.1
  52.4 0.9 copy-done.1
  53.4 0.5 multiply_multiply_fusion
  53.8 0.4 copy-done.6
  54.3 0.1 copy-done.7
  54.3 2.3 add_convert_fusion.6
  56.6 3.3 %add_convert_fusion.1 = (bf16[256,12,28]{2,0,1:T(8,128)(2,1)}, bf16[256,12,28]{2,0,1:T(8,128)(2,1)}, bf16[256,12,28]{2,0,1:T(8,128)(2,1)}, bf16[256,12,28]{2,0,1:T(8,128)(2,1)}) fusion(f32[256,12,128]{2,0,1:T(8,128)S(1)} %multiply_multiply_fusion, f32[256,28]{1,0:T(8,128)S(1)} %get-tuple-element.34, f32[256,28]{1,0:T(8,128)S(1)} %get-tuple-element.33, ...), kind=kLoop, calls=%fused_computation.23 | loop fusion | flops 1376256 | bytes 2179072 | tf_op jit(solution)/shard_map/convert.7
  59.9 5.5 %concatenate.12 = bf16[256,12,128]{2,0,1:T(8,128)(2,1)} concatenate(bf16[256,12,8]{2,0,1:T(8,128)(2,1)S(1)} %get-tuple-element.25, bf16[256,12,8]{2,0,1:T(8,128)(2,1)S(1)} %get-tuple-element.26, bf16[256,12,28]{2,0,1:T(8,128)(2,1)} %get-tuple-element.23, bf16[256,12,28]{2,0,1:T(8,128)(2,1)} %get-tuple-element.24, bf16[256,12,28]{2,0,1:T(8,128)(2,1)} %get-tuple-element.16, ...), dimensions={2} | concatenate | bytes 1572864 | tf_op jit(solution)/shard_map/concatenate | solution.py:38
  65.4 1.4 copy.32
  66.8 0.3 copy.33
  67.1 1.2 slice_bitcast_fusion
  68.3 1.3 pad_maximum_fusion
  69.6 0.0 all-gather.4.cloned.1.call-update
  69.6 0.0 copy-start.9
  69.7 0.0 all-gather.6.cloned.1.call-start
  69.7 0.7 all-gather.6.cloned.1.call-update
  70.4 0.0 reduce-scatter.5.cloned.1.call-start
  71.2 15.0 %all-gather = bf16[1,1,64,1536]{3,2,1,0:T(8,128)(2,1)S(1)} all-gather(bf16[1,1,16,1536]{3,2,1,0:T(8,128)(2,1)S(1)} %slice-done), channel_id=2, replica_groups=mesh['groups'=2,'seq'=4,'tensor'=2,'cfg'=2] {'seq'}, dimensions={2}, use_global_device_ids=true | all-gather | bytes 245760 | tf_op jit(solution)/shard_map/all_gather | solution.py:100
  86.2 0.9 reshape.268
  87.0 0.1 reduce_sum.67
  87.2 0.1 mul.443
  87.3 21.0 %all_gather.13 = bf16[64,1536]{1,0:T(8,128)(2,1)} all-gather(bf16[16,1536]{1,0:T(8,128)(2,1)S(1)} %fusion.28), channel_id=1, replica_groups=mesh['groups'=2,'seq'=4,'tensor'=2,'cfg'=2] {'seq'}, dimensions={0}, use_global_device_ids=true | all-gather | bytes 245760 | tf_op jit(solution)/shard_map/all_gather | solution.py:99
  108.4 4.4 %add_convert_fusion.4 = (bf16[256,12,28]{2,0,1:T(8,128)(2,1)}, bf16[256,12,28]{2,0,1:T(8,128)(2,1)}, bf16[256,12,28]{2,0,1:T(8,128)(2,1)}, bf16[256,12,28]{2,0,1:T(8,128)(2,1)}) fusion(f32[256,12,128]{2,0,1:T(8,128)S(1)} %multiply_multiply_fusion.1, f32[256,28]{1,0:T(8,128)S(1)} %get-tuple-element.34, f32[256,28]{1,0:T(8,128)S(1)} %get-tuple-element.33, ...), kind=kLoop, calls=%fused_computation.31 | loop fusion | flops 1376256 | bytes 2179072 | tf_op jit(solution)/shard_map/convert.13
  112.8 4.6 %concatenate.11 = bf16[256,12,128]{2,0,1:T(8,128)(2,1)S(1)} concatenate(bf16[256,12,8]{2,0,1:T(8,128)(2,1)S(1)} %copy-done.4, bf16[256,12,8]{2,0,1:T(8,128)(2,1)S(1)} %copy-done.3, bf16[256,12,28]{2,0,1:T(8,128)(2,1)} %get-tuple-element.21, bf16[256,12,28]{2,0,1:T(8,128)(2,1)} %get-tuple-element.22, bf16[256,12,28]{2,0,1:T(8,128)(2,1)} %get-tuple-element.10, ...), dimensions={2} | concatenate | bytes 1572864 | tf_op jit(solution)/shard_map/concatenate | solution.py:38
  117.3 1.2 fusion.33
  118.5 71.4 %all-gather.4.cloned.1.call-done = bf16[1024,3072]{1,0:T(8,128)(2,1)} async-done(((bf16[256,3072]{1,0:T(8,128)(2,1)}), bf16[1024,3072]{1,0:T(8,128)(2,1)}) %all-gather.4.cloned.1.call-update) | async-done | bytes 6291472 | tf_op jit(solution)/shard_map/all_gather | solution.py:95
  189.9 4.9 %fusion.30 = (bf16[1024,1536]{1,0:T(8,128)(2,1)S(1)}, bf16[1024,1536]{1,0:T(8,128)(2,1)}) fusion(bf16[1024,3072]{1,0:T(8,128)(2,1)} %all-gather.4.cloned.1.call-done), kind=kLoop, calls=%fused_computation.85 | loop fusion | bytes 12582912 | tf_op jit(solution)/shard_map/split | solution.py:94
  194.8 4.9 %copy.36 = bf16[1024,1536]{0,1:T(8,128)(2,1)} copy(bf16[1024,1536]{1,0:T(8,128)(2,1)} %get-tuple-element.6) | data formatting | bytes 6291456 | tf_op jit(solution)/shard_map/split | solution.py:94
  199.8 2.9 %copy.34 = bf16[1024,1536]{0,1:T(8,128)(2,1)} copy(bf16[1024,1536]{1,0:T(8,128)(2,1)S(1)} %get-tuple-element.5) | data formatting | bytes 6291456 | tf_op jit(solution)/shard_map/split | solution.py:94
  202.7 4.3 %fusion.2 = (f32[12,256]{1,0:T(8,128)S(1)}, f32[12,256,1024]{2,1,0:T(8,128)S(1)}) fusion(bf16[256,12,128]{2,0,1:T(8,128)(2,1)} %copy-done.2, bf16[1024,12,128]{0,2,1:T(8,128)(2,1)} %bitcast.79), kind=kOutput, calls=%fused_computation.3 | convolution fusion | flops 811594752 | bytes 16527360 | tf_op jit(solution)/shard_map/thd,nhd->htn/dot_general | solution.py:79
  207.0 5.3 %fusion.4 = f32[12,256,128]{1,2,0:T(8,128)} fusion(bf16[1024,12,128]{0,2,1:T(8,128)(2,1)} %bitcast.80, f32[12,256,1024]{2,1,0:T(8,128)S(1)} %get-tuple-element.44), kind=kOutput, calls=%fused_computation.5 | convolution fusion | flops 811597824 | bytes 17301504 | tf_op jit(solution)/shard_map/htn,nhd->htd/dot_general | solution.py:84
  212.3 2.0 fusion.17
  214.2 0.0 all-gather.6.cloned.1.call-done
  214.3 7.5 %convolution_convert_fusion = bf16[256,3072]{1,0:T(8,128)(2,1)} fusion(bf16[256,1536]{0,1:T(8,128)(2,1)S(1)} %bitcast.82, bf16[1536,3072]{1,0:T(8,128)(2,1)} %all-gather.6.cloned.1.call-done), kind=kOutput, calls=%fused_computation.10 | convolution fusion | flops 2416705536 | bytes 11796480 | tf_op jit(solution)/shard_map/dot_general | solution.py:115
  221.7 0.0 reduce-scatter.5.cloned.1.call-update
  221.8 0.7 copy-done.11
  222.5 25.0 %reduce-scatter.5.cloned.1.call-done = bf16[128,3072]{1,0:T(8,128)(2,1)} async-done(((bf16[256,3072]{1,0:T(8,128)(2,1)}), bf16[128,3072]{1,0:T(8,128)(2,1)}) %reduce-scatter.5.cloned.1.call-update) | async-done | bytes 786448 | tf_op jit(solution)/shard_map/reduce_scatter | solution.py:114
  247.5 1.3 multiply_convert_fusion
  248.8 0.1 collective-permute-start
  249.5 1.1 collective-permute-done
  250.6 0.9 fusion.21
  (45 shorter events, 0.3 us)
Async XLA Ops:
  6.5 3.2 %copy-start = (bf16[256,3072]{1,0:T(8,128)(2,1)S(1)}, bf16[256,3072]{1,0:T(8,128)(2,1)}, u32[]{:S(2)}) copy-start(bf16[256,3072]{1,0:T(8,128)(2,1)} %param.9) | copy-start | bytes 4718596
  6.5 37.2 %reduce-scatter.3.cloned.1.call-start = ((), (), s32[]{:S(2)}) async-start(), calls=%async_computation.2 | async-start | bytes 7077888 | tf_op jit(solution)/shard_map/reduce_scatter | solution.py:56
  28.3 0.7 copy-start.13
  28.3 2.4 copy-start.15
  28.3 161.6 %all-gather.4.cloned.1.call-start = ((), (), s32[]{:S(2)}) async-start(), calls=%async_computation.3 | async-start | bytes 7864320 | tf_op jit(solution)/shard_map/all_gather | solution.py:95
  51.3 0.6 copy-start.14
  51.9 1.4 copy-start.1
  51.9 1.4 copy-start.12
  53.3 0.9 copy-start.6
  53.4 1.0 copy-start.7
  54.3 2.3 copy-start.5
  69.6 1.5 copy-start.9
  69.6 1.5 slice-start
  69.7 144.6 %all-gather.6.cloned.1.call-start = ((), (), s32[]{:S(2)}) async-start(), calls=%async_computation.4 | async-start | bytes 14155776 | tf_op jit(solution)/shard_map/all_gather | solution.py:113
  70.4 177.1 %reduce-scatter.5.cloned.1.call-start = ((), (), s32[]{:S(2)}) async-start(), calls=%async_computation.5 | async-start | bytes 2359296 | tf_op jit(solution)/shard_map/reduce_scatter | solution.py:114
  108.3 4.4 %copy-start.3 = (bf16[256,12,8]{2,0,1:T(8,128)(2,1)S(1)}, bf16[256,12,8]{2,0,1:T(8,128)(2,1)}, u32[]{:S(2)}) copy-start(bf16[256,12,8]{2,0,1:T(8,128)(2,1)} %get-tuple-element.13) | copy-start | bytes 147460
  108.3 4.4 %copy-start.4 = (bf16[256,12,8]{2,0,1:T(8,128)(2,1)S(1)}, bf16[256,12,8]{2,0,1:T(8,128)(2,1)}, u32[]{:S(2)}) copy-start(bf16[256,12,8]{2,0,1:T(8,128)(2,1)} %get-tuple-element.14) | copy-start | bytes 147460
  112.8 4.6 %copy-start.10 = (bf16[64,1536]{1,0:T(8,128)(2,1)S(1)}, bf16[64,1536]{1,0:T(8,128)(2,1)}, u32[]{:S(2)}) copy-start(bf16[64,1536]{1,0:T(8,128)(2,1)} %all_gather.13) | copy-start | bytes 589828
  117.3 1.2 copy-start.2
  207.0 5.3 %copy-start.8 = (bf16[64,12,128]{2,1,0:T(8,128)(2,1)S(1)}, bf16[64,12,128]{2,1,0:T(8,128)(2,1)}, u32[]{:S(2)}) copy-start(bf16[64,12,128]{2,1,0:T(8,128)(2,1)} %reshape.268) | copy-start | bytes 589828
  221.7 0.7 copy-start.11
  248.8 1.8 collective-permute-start
Sparse Core Ops, SparseCore 0:
  28.4 15.2 reduce-scatter.2
  69.8 120.1 all-gather.3
  191.5 19.9 all-gather.5
  221.9 25.5 reduce-scatter.4
